TPU v7x, 32 devices: a whole 2x2x4 slice. The times are simulated.
32 devices in a mesh: dp: 8 (over z, x), expert: 4 (over y, core).
Axes of the slice: x: 2, y: 2, z: 4, core: 2. Of those that a mesh axis runs over, the one named last changes fastest.
Arguments:
- tokens: bfloat16 [4096, 2048], P(('dp', 'expert')), may hold values from -6 to 6
- out_grad: bfloat16 [4096, 2048], P(('dp', 'expert')), may hold values from -3 to 3
- z_weight: float32 [4096], P(('dp', 'expert')), may hold values from 0.1 to 1
- router_weight: bfloat16 [2048, 128], replicated, may hold values from -0.125 to 0.125
- expert_ids: int32 [4096, 4], P(('dp', 'expert')), may hold values from 0 to 127, as said below
- gate_up_weight: bfloat16 [4, 2048, 3072], P('expert'), may hold values from -0.125 to 0.125
- down_weight: bfloat16 [4, 1536, 2048], P('expert'), may hold values from -0.15625 to 0.15625
Outputs:
- token_grad: bfloat16 [4096, 2048], P(('dp', 'expert'))
- router_grad: float32 [2048, 128], replicated
- gate_up_grad: bfloat16 [4, 2048, 3072], P('expert', 'dp')
- down_grad: bfloat16 [4, 1536, 2048], P('expert', 'dp')
Inputs may be any that keep to these rules, and one draw needn't show every extreme that they name: `expert_ids`: each row names 4 different experts. Experts 0 to 3 are the ones in flight. The 128 rows of one device name any one expert in flight at most 64 times; in every data group some expert in flight is named exactly 64 times by the rows of each device of the group.
All inputs are finite; a program needn't handle non-finite values.
Results may differ from a plain program's by a relative error of at most 0.019.
Values may be sent and summed in bfloat16 or wider, within the bound.
A program may use at most 192 MiB of HBM per device.

v0:
```python
import jax
import jax.numpy as jnp
from jax import lax
from jax.sharding import PartitionSpec as P


def expert_rows(rows_in, rows_grad, w_gateup, w_down, acc_gateup, acc_down):
    hidden_units = w_down.shape[0]
    pre_act = jnp.dot(rows_in, w_gateup, preferred_element_type=jnp.float32)
    gate_pre = pre_act[:, :hidden_units]
    up_pre = pre_act[:, hidden_units:]
    activated = jax.nn.silu(gate_pre)
    hidden = (activated * up_pre).astype(jnp.bfloat16)
    expert_out = jnp.dot(hidden, w_down, preferred_element_type=jnp.float32).astype(jnp.bfloat16)
    hidden_grad = lax.dot_general(
        rows_grad, w_down, (((1,), (1,)), ((), ())), preferred_element_type=jnp.float32
    )
    acc_down = lax.dot_general(
        hidden, rows_grad, (((0,), (0,)), ((), ())), preferred_element_type=jnp.float32
    )
    sigmoid_gate = jax.nn.sigmoid(gate_pre)
    gate_grad = hidden_grad * up_pre * sigmoid_gate * (1.0 + gate_pre * (1.0 - sigmoid_gate))
    up_grad = hidden_grad * activated
    pre_grad = jnp.concatenate([gate_grad, up_grad], axis=1).astype(jnp.bfloat16)
    acc_gateup = lax.dot_general(
        rows_in, pre_grad, (((0,), (0,)), ((), ())), preferred_element_type=jnp.float32
    )
    input_grad = lax.dot_general(
        pre_grad, w_gateup, (((1,), (1,)), ((), ())), preferred_element_type=jnp.float32
    ).astype(jnp.bfloat16)
    return (acc_gateup, acc_down, expert_out, input_grad)


def split_pair(values):
    upper = values.astype(jnp.bfloat16)
    lower = (values - upper.astype(jnp.float32)).astype(jnp.bfloat16)
    return jnp.stack([upper, lower], axis=-1)


def join_pair(pair):
    return pair[..., 0].astype(jnp.float32) + pair[..., 1].astype(jnp.float32)


def per_device(tokens, out_grad, z_weight, router_weight, expert_ids, gate_up_weight, down_weight):
    tok_count, width = tokens.shape
    top_count = expert_ids.shape[1]
    routed = router_weight.shape[1]
    flight = lax.axis_size("expert")
    capacity = tok_count // 2
    w_gateup = gate_up_weight[0]
    w_down = down_weight[0]
    hidden_units = w_down.shape[0]
    logits = jnp.dot(tokens, router_weight, preferred_element_type=jnp.float32)
    choose = expert_ids[:, :, None] == jnp.arange(routed, dtype=jnp.int32)[None, None, :]
    selected = jnp.sum(jnp.where(choose, logits[:, None, :], 0.0), axis=2)
    sel_exp = jnp.exp(selected)
    probs = sel_exp / jnp.sum(sel_exp, axis=1, keepdims=True)
    log_total = jnp.log(jnp.sum(jnp.exp(logits), axis=1))
    flat_ids = expert_ids.reshape(-1)
    slot_count = tok_count * top_count
    member = (flat_ids[:, None] == jnp.arange(flight, dtype=jnp.int32)[None, :]).astype(jnp.int32)
    ranks = jnp.sum((jnp.cumsum(member, axis=0) - 1) * member, axis=1)
    in_flight = flat_ids < flight
    position = jnp.where(in_flight, flat_ids * capacity + ranks, flight * capacity)
    source_slot = (
        jnp.zeros((flight * capacity,), jnp.int32)
        .at[position]
        .set(jnp.arange(slot_count, dtype=jnp.int32), mode="drop")
    )
    filled = jnp.zeros((flight * capacity,), jnp.bool_).at[position].set(True, mode="drop")
    source_tok = source_slot // top_count
    send_in = jnp.where(filled[:, None], tokens[source_tok], 0)
    slot_prob = jnp.where(filled, probs.reshape(-1)[source_slot], 0.0)
    counts = jnp.sum(member, axis=0)
    count_msg = jnp.stack([counts // 128, counts % 128], axis=1).astype(jnp.bfloat16)
    send_raw = jnp.where(filled[:, None], out_grad[source_tok], 0)
    prob_pair = split_pair(slot_prob)
    recv_in, recv_raw, recv_prob, recv_counts = (
        lax.all_to_all(
            send_in.reshape(flight, capacity, width),
            "expert",
            split_axis=0,
            concat_axis=0,
            tiled=True,
        ),
        lax.all_to_all(
            send_raw.reshape(flight, capacity, width),
            "expert",
            split_axis=0,
            concat_axis=0,
            tiled=True,
        ),
        lax.all_to_all(
            prob_pair.reshape(flight, capacity, 2),
            "expert",
            split_axis=0,
            concat_axis=0,
            tiled=True,
        ),
        lax.all_to_all(count_msg, "expert", split_axis=0, concat_axis=0, tiled=True),
    )
    sources = recv_in.shape[0]
    total_rows = sources * capacity
    flat_in = recv_in.reshape(total_rows, width)
    flat_raw = recv_raw.reshape(total_rows, width)
    row_prob = join_pair(recv_prob.reshape(total_rows, 2))
    flat_grad = (row_prob[:, None] * flat_raw.astype(jnp.float32)).astype(jnp.bfloat16)
    acc_gateup, acc_down, produced, back_rows = expert_rows(
        flat_in,
        flat_grad,
        w_gateup,
        w_down,
        jnp.zeros((width, 2 * hidden_units), jnp.float32),
        jnp.zeros((hidden_units, width), jnp.float32),
    )
    slot_at = jnp.where(in_flight, position, 0)
    row_score = jnp.sum(flat_raw.astype(jnp.float32) * produced.astype(jnp.float32), axis=1)
    score_pair = split_pair(row_score)
    home_dx, home_pair = (
        lax.all_to_all(
            back_rows.reshape(sources, capacity, width),
            "expert",
            split_axis=0,
            concat_axis=0,
            tiled=True,
        ),
        lax.all_to_all(
            score_pair.reshape(sources, capacity, 2),
            "expert",
            split_axis=0,
            concat_axis=0,
            tiled=True,
        ),
    )
    flat_dx = home_dx.reshape(flight * capacity, width)
    flat_score = join_pair(home_pair.reshape(flight * capacity, 2))
    scores = jnp.where(in_flight, flat_score[slot_at], 0.0).reshape(tok_count, top_count)
    slot_dx = jnp.where(in_flight[:, None], flat_dx[slot_at], 0).reshape(
        tok_count, top_count, width
    )
    mean_score = jnp.sum(probs * scores, axis=1, keepdims=True)
    sel_grad = probs * (scores - mean_score)
    z_grad = 2.0 * z_weight[:, None] * log_total[:, None] * jnp.exp(logits - log_total[:, None])
    logit_grad = (z_grad + jnp.sum(jnp.where(choose, sel_grad[:, :, None], 0.0), axis=1)).astype(
        jnp.bfloat16
    )
    token_grad = (
        jnp.sum(slot_dx.astype(jnp.float32), axis=1)
        + lax.dot_general(
            logit_grad, router_weight, (((1,), (1,)), ((), ())), preferred_element_type=jnp.float32
        )
    ).astype(jnp.bfloat16)
    router_part = lax.dot_general(
        tokens, logit_grad, (((0,), (0,)), ((), ())), preferred_element_type=jnp.float32
    )
    router_grad = lax.psum(router_part, ("dp", "expert"))
    part_gateup = acc_gateup.astype(jnp.bfloat16)
    part_down = acc_down.astype(jnp.bfloat16)
    gate_up_grad, down_grad = (
        lax.psum_scatter(part_gateup[None], "dp", scatter_dimension=1, tiled=True).astype(
            jnp.float32
        ),
        lax.psum_scatter(part_down[None], "dp", scatter_dimension=1, tiled=True).astype(
            jnp.float32
        ),
    )
    return (
        token_grad,
        router_grad,
        gate_up_grad.astype(jnp.bfloat16),
        down_grad.astype(jnp.bfloat16),
    )


def solution(mesh):
    return jax.shard_map(
        per_device,
        mesh=mesh,
        in_specs=(
            P(("dp", "expert"), None),
            P(("dp", "expert"), None),
            P(("dp", "expert")),
            P(),
            P(("dp", "expert"), None),
            P("expert", None, None),
            P("expert", None, None),
        ),
        out_specs=(
            P(("dp", "expert"), None),
            P(),
            P("expert", "dp", None),
            P("expert", "dp", None),
        ),
        check_vma=False,
    )
```

profile of v0, /device:TPU:0, one launch (start us, length us, event | category | flops | bytes accessed | tf_op | source)
XLA Modules:
  0.0 440.1 jit_solution(1820209398362379599)
XLA Ops:
  8.0 0.7 broadcast_compare_fusion
  8.8 0.7 broadcast_multiply_fusion
  9.4 0.8 copy.45
  10.6 0.6 copy-done.5
  11.5 1.2 reduce-window.6
  13.3 2.4 scatter_custom_fusion.1
  15.8 2.4 scatter_custom_fusion
  18.3 0.6 pad_clamp_fusion.1
  18.9 1.4 gather_fusion.2
  20.3 1.4 gather_fusion.1
  21.7 1.5 broadcast_select_fusion
  23.2 4.4 all-to-all-start.2
  28.3 0.6 multiply_multiply_fusion
  29.0 13.1 %all-to-all-done.2 = bf16[4,64,2048]{2,1,0:T(8,128)(2,1)S(1)} async-done(((bf16[4,64,2048]{2,1,0:T(8,128)(2,1)}), bf16[4,64,2048]{2,1,0:T(8,128)(2,1)S(1)}, u32[]{:S(2)}, u32[]{:S(2)}) %all-to-all-start.2) | async-done | bytes 1048608 | tf_op jit(solution)/shard_map/all_to_all | solution.py:79
  42.0 3.5 all-to-all-start.1
  45.6 9.7 %fusion.2 = f32[256,3072]{1,0:T(8,128)} fusion(bf16[256,2048]{1,0:T(8,128)(2,1)S(1)} %bitcast.81, bf16[1,2048,3072]{2,1,0:T(8,128)(2,1)} %param.12), kind=kOutput, calls=%fused_computation.9 | convolution fusion | flops 3221225472 | bytes 16777216 | tf_op jit(solution)/shard_map/dot_general | solution.py:9
  55.2 2.3 multiply_convert_fusion.1
  57.6 2.4 all-to-all-done.1
  60.0 4.8 %fusion.24 = f32[256]{0:T(256)S(1)} fusion(bf16[256,1536]{1,0:T(8,128)(2,1)S(1)} %multiply_convert_fusion.1, bf16[1,1536,2048]{2,1,0:T(8,128)(2,1)} %param.13, bf16[256,2048]{1,0:T(8,128)(2,1)S(1)} %bitcast.80), kind=kOutput, calls=%fused_computation.35 | convolution fusion | flops 1613233920 | bytes 8127488 | tf_op jit(solution)/shard_map/dot_general | solution.py:14
  64.8 0.6 copy.51
  65.4 3.4 all-to-all-start.4
  68.8 0.5 exponential_reduce_fusion.1
  69.4 3.0 all-to-all-done.4
  72.4 3.5 gather_fusion.4
  76.1 1.2 multiply_reduce_fusion
  77.3 0.6 copy-done.8
  78.1 2.1 gather_fusion
  80.2 0.6 subtract_convert_fusion.1
  80.8 0.6 select_convert_fusion
  81.4 0.7 subtract_multiply_fusion
  82.2 0.6 copy.49
  82.8 3.2 all-to-all-start
  86.3 0.7 copy.54
  87.0 0.9 add_convert_fusion
  87.9 1.3 convolution_bitcast_fusion
  90.3 0.7 fusion.38
  91.2 4.4 %fusion.4 = bf16[1,1536,2048]{2,1,0:T(8,128)(2,1)} fusion(bf16[256,1536]{1,0:T(8,128)(2,1)S(1)} %multiply_convert_fusion.1, bf16[256,2048]{1,0:T(8,128)(2,1)S(1)} %fusion.22), kind=kOutput, calls=%fused_computation.13 | convolution fusion | flops 1613758464 | bytes 8126464 | tf_op jit(solution)/shard_map/dot_general | solution.py:18
  96.1 6.0 %multiply_convert_fusion.3 = (bf16[256,1536]{1,0:T(8,128)(2,1)S(1)}, bf16[256,1536]{1,0:T(8,128)(2,1)S(1)}) fusion(f32[256,3072]{1,0:T(8,128)} %fusion.2, bf16[256,2048]{1,0:T(8,128)(2,1)S(1)} %bitcast.85, bf16[1,1536,2048]{2,1,0:T(8,128)(2,1)} %param.13), kind=kOutput, calls=%fused_computation.32 | convolution fusion | flops 1615724544 | bytes 12058624 | tf_op jit(solution)/shard_map/dot_general | solution.py:15
  102.1 6.6 %convert_bitcast_fusion = bf16[1,2048,3072]{2,1,0:T(8,128)(2,1)} fusion(bf16[256,2048]{1,0:T(8,128)(2,1)S(1)} %bitcast.82, bf16[256,1536]{1,0:T(8,128)(2,1)S(1)} %get-tuple-element.31, bf16[256,1536]{1,0:T(8,128)(2,1)S(1)} %get-tuple-element.30), kind=kOutput, calls=%fused_computation.11 | convolution fusion | flops 3230662656 | bytes 15204352 | tf_op jit(solution)/shard_map/dot_general | solution.py:25
  108.7 9.0 %fusion.18 = bf16[256,2048]{1,0:T(8,128)(2,1)} fusion(bf16[1,2048,3072]{2,1,0:T(8,128)(2,1)} %param.12, bf16[256,1536]{1,0:T(8,128)(2,1)S(1)} %get-tuple-element.31, bf16[256,1536]{1,0:T(8,128)(2,1)S(1)} %get-tuple-element.30), kind=kOutput, calls=%fused_computation.22 | convolution fusion | flops 3224895488 | bytes 15204352 | tf_op jit(solution)/shard_map/dot_general | solution.py:28
  117.8 3.9 all-to-all-start.3
  121.7 229.6 %all-reduce.2.cloned.1.call-done = f32[2048,128]{0,1:T(8,128)} async-done(((f32[2048,128]{0,1:T(8,128)}), f32[2048,128]{0,1:T(8,128)}) %all-reduce.2.cloned.1.call-update) | async-done | bytes 1048592 | tf_op jit(solution)/shard_map/psum | solution.py:156
  351.2 2.6 copy.55
  353.8 2.5 gather_fusion.3
  356.3 2.2 gather.29
  358.6 5.6 %convert_reduce_fusion = f32[128,2048]{1,0:T(8,128)S(1)} fusion(bf16[128,4,2048]{2,1,0:T(4,128)(2,1)} %gather.29, pred[128,4]{1,0:T(8,128)(4,1)S(1)} %copy-done.6), kind=kLoop, calls=%fused_computation.18 | loop fusion | flops 2883584 | bytes 3146240 | tf_op jit(solution)/shard_map/reduce_sum | solution.py:148
  364.1 1.1 fusion.21
  365.3 67.3 %reduce-scatter.3.cloned.1.call-done = bf16[1,256,3072]{2,1,0:T(8,128)(2,1)} async-done(((bf16[1,2048,3072]{2,1,0:T(8,128)(2,1)}), bf16[1,256,3072]{2,1,0:T(8,128)(2,1)}) %reduce-scatter.3.cloned.1.call-update) | async-done | bytes 1572880 | tf_op jit(solution)/shard_map/reduce_scatter | solution.py:160
  (73 shorter events, 4.8 us)
Async XLA Ops:
  8.0 10.9 %copy-start = (bf16[128,2048]{1,0:T(8,128)(2,1)S(1)}, bf16[128,2048]{1,0:T(8,128)(2,1)}, u32[]{:S(2)}) copy-start(bf16[128,2048]{1,0:T(8,128)(2,1)} %param.7) | copy-start | bytes 1572868
  10.6 0.6 copy-start.5
  18.2 0.7 copy-start.11
  18.9 1.4 copy-start.2
  23.2 4.4 %copy-start.3 = (bf16[2048,128]{1,0:T(8,128)(2,1)S(1)}, bf16[2048,128]{1,0:T(8,128)(2,1)}, u32[]{:S(2)}) copy-start(bf16[2048,128]{1,0:T(8,128)(2,1)} %param.10) | copy-start | bytes 1572868
  23.2 4.9 %copy-start.7 = (s32[128,4]{0,1:T(4,128)S(1)}, s32[128,4]{0,1:T(4,128)}, u32[]{:S(2)}) copy-start(s32[128,4]{0,1:T(4,128)} %param.11) | copy-start | bytes 6148
  23.2 5.1 %copy-start.12 = (f32[128]{0:T(128)S(1)}, f32[128]{0:T(128)}, u32[]{:S(2)}) copy-start(f32[128]{0:T(128)} %param.9) | copy-start | bytes 1540
  23.2 18.8 %all-to-all-start.2 = ((bf16[4,64,2048]{2,1,0:T(8,128)(2,1)}), bf16[4,64,2048]{2,1,0:T(8,128)(2,1)S(1)}, u32[]{:S(2)}, u32[]{:S(2)}) async-start(bf16[4,64,2048]{2,1,0:T(8,128)(2,1)} %get-tuple-element.38), calls=%async_computation.2 | async-start | bytes 2097152 | tf_op jit(solution)/shard_map/all_to_all | solution.py:79
  28.1 44.3 %copy-start.9 = (s32[1024]{0:T(1024)}, s32[1024]{0:T(1024)S(1)}, u32[]{:S(2)}) copy-start(s32[1024]{0:T(1024)S(1)} %pad_clamp_fusion) | copy-start | bytes 12292
  42.0 17.9 %all-to-all-start.1 = ((bf16[4,64,2048]{2,1,0:T(8,128)(2,1)}), bf16[4,64,2048]{2,1,0:T(8,128)(2,1)S(1)}, u32[]{:S(2)}, u32[]{:S(2)}) async-start(bf16[4,64,2048]{2,1,0:T(8,128)(2,1)} %get-tuple-element.39), calls=%async_computation.1 | async-start | bytes 2097152 | tf_op jit(solution)/shard_map/all_to_all | solution.py:86
  65.4 6.9 %all-to-all-start.4 = ((bf16[4,64,2]{1,2,0:T(2,128)(2,1)}), bf16[4,64,2]{1,2,0:T(2,128)(2,1)S(1)}, u32[]{:S(2)}, u32[]{:S(2)}) async-start(bf16[4,64,2]{1,2,0:T(2,128)(2,1)} %copy.51), calls=%async_computation.4 | async-start | bytes 4096 | tf_op jit(solution)/shard_map/all_to_all | solution.py:127
  77.3 0.6 copy-start.8
  82.8 6.9 %all-to-all-start = ((bf16[4,64,2]{1,2,0:T(2,128)(2,1)}), bf16[4,64,2]{1,2,0:T(2,128)(2,1)S(1)}, u32[]{:S(2)}, u32[]{:S(2)}) async-start(bf16[4,64,2]{1,2,0:T(2,128)(2,1)} %copy.49), calls=%async_computation | async-start | bytes 4096 | tf_op jit(solution)/shard_map/all_to_all | solution.py:93
  86.0 265.2 %all-reduce.2.cloned.1.call-start = ((), (), s32[]{:S(2)}) async-start(), calls=%async_computation.7 | async-start | bytes 2097152 | tf_op jit(solution)/shard_map/psum | solution.py:156
  89.2 276.1 %reduce-scatter.5.cloned.1.call-start = ((), (), s32[]{:S(2)}) async-start(), calls=%async_computation.9 | async-start | bytes 7077888 | tf_op jit(solution)/shard_map/reduce_scatter | solution.py:163
  95.7 336.9 %reduce-scatter.3.cloned.1.call-start = ((), (), s32[]{:S(2)}) async-start(), calls=%async_computation.8 | async-start | bytes 14155776 | tf_op jit(solution)/shard_map/reduce_scatter | solution.py:160
  117.8 236.0 %copy-start.10 = (s32[1024]{0:T(1024)S(1)}, s32[1024]{0:T(1024)}, u32[]{:S(2)}) copy-start(s32[1024]{0:T(1024)} %copy-done.9) | copy-start | bytes 12292
  117.8 236.0 %all-to-all-start.3 = ((bf16[4,64,2048]{2,1,0:T(8,128)(2,1)}), bf16[4,64,2048]{2,1,0:T(8,128)(2,1)S(1)}, u32[]{:S(2)}, u32[]{:S(2)}) async-start(bf16[4,64,2048]{2,1,0:T(8,128)(2,1)} %bitcast.9), calls=%async_computation.3 | async-start | bytes 2097152 | tf_op jit(solution)/shard_map/all_to_all | solution.py:120
  356.3 2.3 copy-start.6
  356.3 76.3 %copy-start.1 = (bf16[128,2048]{1,0:T(8,128)(2,1)S(1)}, bf16[128,2048]{1,0:T(8,128)(2,1)}, u32[]{:S(2)}) copy-start(bf16[128,2048]{1,0:T(8,128)(2,1)} %param.7) | copy-start | bytes 1572868
  358.6 5.6 %copy-start.4 = (bf16[2048,128]{1,0:T(8,128)(2,1)S(1)}, bf16[2048,128]{1,0:T(8,128)(2,1)}, u32[]{:S(2)}) copy-start(bf16[2048,128]{1,0:T(8,128)(2,1)} %param.10) | copy-start | bytes 1572868
Sparse Core Ops, SparseCore 0:
  92.6 258.5 all-reduce.1
Sparse Core Ops, SparseCore 1:
  95.8 123.6 reduce-scatter.4
  223.5 209.1 reduce-scatter.2
where the time goes:
time: 441 us; the launch traced here: 440 us
  waiting for transfers between devices  316 us (72%)
  matrix products  43.3 us (10%)
  local copies, waits for them, and re-layouts  26.9 us (6%)
  other arithmetic  19.7 us (4%)
  starting transfers between devices  18.5 us (4%)
  between operations  15.8 us (4%)
    psum x1, waiting for transfers between devices, per_device(): router_grad = lax.psum(router_part, ('dp', 'expert'))  230 us
    reduce_scatter x1, waiting for transfers between devices, per_device(): lax.psum_scatter(part_gateup[None], 'dp', scatter_dimension=1, tiled=True)  67.3 us
    all_to_all x1, waiting for transfers between devices, per_device(): lax.all_to_all(send_in.reshape(flight, capacity, width), 'expert', split_...  13.1 us
    dot_general x1, matrix products, expert_rows(): pre_act = jnp.dot(rows_in, w_gateup, preferred_element_type=jnp.float32)  9.69 us
    dot_general x1, matrix products, expert_rows(): lax.dot_general(pre_grad, w_gateup, (((1,), (1,)), ((), ())), preferred_e...  9.05 us
  transfers between devices with their start and end apart: 8, of which 6 were waited for; matrix products, arithmetic and copies ran while one was open for 13% of the time, Pallas kernels for 0%

commit v1 on v0

--- a/solution.py
+++ b/solution.py
@@ -153,7 +153,7 @@
     router_part = lax.dot_general(
         tokens, logit_grad, (((0,), (0,)), ((), ())), preferred_element_type=jnp.float32
     )
-    router_grad = lax.psum(router_part, ("dp", "expert"))
+    router_grad = lax.psum(lax.psum(router_part, "expert"), "dp")
     part_gateup = acc_gateup.astype(jnp.bfloat16)
     part_down = acc_down.astype(jnp.bfloat16)
     gate_up_grad, down_grad = (

time: 441 us -> 539 us (1.22)
  waiting for transfers between devices: 316 us -> 404 us
  blocking collectives: 0 us -> 23 us
  starting transfers between devices: 18.5 us -> 11.5 us
    psum x1 -> x2, waiting for transfers between devices: 230 us -> 55.6 us  [per_device(): router_grad = lax.psum(lax.psum(router_part, 'expert'), 'dp')]
    reduce_scatter x1, waiting for transfers between devices: 67.3 us -> 211 us  [per_device(): lax.psum_scatter(part_gateup[None], 'dp', scatter_dimension=1, tiled=True)]
    reduce_scatter x1, waiting for transfers between devices: 0.01 us -> 119 us  [per_device(): lax.psum_scatter(part_down[None], 'dp', scatter_dimension=1, tiled=True)]
    all_to_all x0 -> x2, blocking collectives: none -> 23 us  [the longest x1 16.9 us: per_device(): lax.all_to_all(back_rows.reshape(sources, capacity, width), 'expert', spl...]
    all_to_all x2 -> x0, starting transfers between devices: 7.09 us -> none  [the longest x1 3.87 us: per_device(): lax.all_to_all(back_rows.reshape(sources, capacity, width), 'expert', spl...]
  transfers between devices with their start and end apart: 8 -> 7, of which waited for: 6 -> 7; matrix products, arithmetic and copies ran while one was open for 13% -> 11% of each run, Pallas kernels for 0% -> 0%
where the time goes in v1:
time: 539 us; the launch traced here: 538 us
  waiting for transfers between devices  404 us (75%)
  matrix products  42.4 us (8%)
  local copies, waits for them, and re-layouts  25.7 us (5%)
  blocking collectives  23 us (4%)
  other arithmetic  17.3 us (3%)
  between operations  14.1 us (3%)
  starting transfers between devices  11.5 us (2%)
    reduce_scatter x1, waiting for transfers between devices, per_device(): lax.psum_scatter(part_gateup[None], 'dp', scatter_dimension=1, tiled=True)  211 us
    reduce_scatter x1, waiting for transfers between devices, per_device(): lax.psum_scatter(part_down[None], 'dp', scatter_dimension=1, tiled=True)  119 us
    psum x2, waiting for transfers between devices, per_device(): router_grad = lax.psum(lax.psum(router_part, 'expert'), 'dp')  55.6 us
    all_to_all x1, blocking collectives, per_device(): lax.all_to_all(back_rows.reshape(sources, capacity, width), 'expert', spl...  16.9 us
    all_to_all x1, waiting for transfers between devices, per_device(): lax.all_to_all(send_in.reshape(flight, capacity, width), 'expert', split_...  13.1 us
  transfers between devices with their start and end apart: 7, of which 7 were waited for; matrix products, arithmetic and copies ran while one was open for 11% of the time, Pallas kernels for 0%

profile of v1, /device:TPU:0, one launch (start us, length us, event | category | flops | bytes accessed | tf_op | source)
XLA Modules:
  0.0 538.0 jit_solution(5868426447416874383)
XLA Ops:
  7.2 0.7 broadcast_compare_fusion
  7.9 0.7 broadcast_multiply_fusion
  8.6 0.8 copy.45
  9.8 0.6 copy-done.5
  10.7 1.2 reduce-window.6
  12.5 2.4 scatter_custom_fusion.1
  14.9 2.4 scatter_custom_fusion
  17.5 0.6 pad_clamp_fusion.1
  18.1 1.4 gather_fusion.2
  19.5 1.4 gather_fusion.1
  20.8 1.5 broadcast_select_fusion
  22.4 4.4 all-to-all-start.2
  26.8 0.4 exponential_reduce_fusion
  27.5 0.5 multiply_multiply_fusion
  28.1 13.1 %all-to-all-done.2 = bf16[4,64,2048]{2,1,0:T(8,128)(2,1)S(1)} async-done(((bf16[4,64,2048]{2,1,0:T(8,128)(2,1)}), bf16[4,64,2048]{2,1,0:T(8,128)(2,1)S(1)}, u32[]{:S(2)}, u32[]{:S(2)}) %all-to-all-start.2) | async-done | bytes 1048608 | tf_op jit(solution)/shard_map/all_to_all | solution.py:79
  41.2 3.5 all-to-all-start.1
  44.7 9.7 %fusion.2 = f32[256,3072]{1,0:T(8,128)} fusion(bf16[256,2048]{1,0:T(8,128)(2,1)S(1)} %bitcast.81, bf16[1,2048,3072]{2,1,0:T(8,128)(2,1)} %param.12), kind=kOutput, calls=%fused_computation.9 | convolution fusion | flops 3221225472 | bytes 16777216 | tf_op jit(solution)/shard_map/dot_general | solution.py:9
  54.4 2.3 multiply_convert_fusion.1
  56.7 2.4 all-to-all-done.1
  59.1 4.8 fusion.24
  64.0 0.6 copy.51
  64.6 3.2 all-to-all-start.4
  68.0 0.5 exponential_reduce_fusion.1
  68.6 2.9 all-to-all-done.4
  71.6 3.5 gather_fusion.4
  75.3 0.7 multiply_reduce_fusion
  76.2 0.7 copy.54
  76.9 0.9 add_convert_fusion
  77.8 1.3 convolution_bitcast_fusion
  79.3 2.1 gather_fusion
  81.6 34.9 %all-reduce.3.cloned.1.call-done = f32[2048,128]{0,1:T(8,128)} async-done(((f32[2048,128]{0,1:T(8,128)}), f32[2048,128]{0,1:T(8,128)}) %all-reduce.3.cloned.1.call-update) | async-done | bytes 1048592 | tf_op jit(solution)/shard_map/psum | solution.py:156
  116.6 6.1 %all_to_all.25 = bf16[4,64,2]{1,2,0:T(2,128)(2,1)S(1)} all-to-all(bf16[4,64,2]{1,2,0:T(2,128)(2,1)S(1)} %copy.49), channel_id=1, replica_groups=mesh['dp'=8,'expert'=4] {'expert'}, dimensions={0} | all-to-all | bytes 2048 | tf_op jit(solution)/shard_map/all_to_all | solution.py:93
  122.8 0.5 broadcast.186
  123.3 0.7 fusion.38
  124.3 4.4 fusion.4
  128.9 0.2 multiply_convert_fusion
  129.1 6.0 %multiply_convert_fusion.3 = (bf16[256,1536]{1,0:T(8,128)(2,1)S(1)}, bf16[256,1536]{1,0:T(8,128)(2,1)S(1)}) fusion(f32[256,3072]{1,0:T(8,128)} %fusion.2, bf16[256,2048]{1,0:T(8,128)(2,1)S(1)} %bitcast.85, bf16[1,1536,2048]{2,1,0:T(8,128)(2,1)} %param.13), kind=kOutput, calls=%fused_computation.32 | convolution fusion | flops 1615724544 | bytes 12058624 | tf_op jit(solution)/shard_map/dot_general | solution.py:15
  135.2 6.7 %convert_bitcast_fusion = bf16[1,2048,3072]{2,1,0:T(8,128)(2,1)} fusion(bf16[256,2048]{1,0:T(8,128)(2,1)S(1)} %bitcast.82, bf16[256,1536]{1,0:T(8,128)(2,1)S(1)} %get-tuple-element.31, bf16[256,1536]{1,0:T(8,128)(2,1)S(1)} %get-tuple-element.30), kind=kOutput, calls=%fused_computation.11 | convolution fusion | flops 3230662656 | bytes 15204352 | tf_op jit(solution)/shard_map/dot_general | solution.py:25
  141.8 8.0 %fusion.18 = bf16[256,2048]{1,0:T(8,128)(2,1)S(1)} fusion(bf16[1,2048,3072]{2,1,0:T(8,128)(2,1)} %param.12, bf16[256,1536]{1,0:T(8,128)(2,1)S(1)} %get-tuple-element.31, bf16[256,1536]{1,0:T(8,128)(2,1)S(1)} %get-tuple-element.30), kind=kOutput, calls=%fused_computation.22 | convolution fusion | flops 3224895488 | bytes 15204352 | tf_op jit(solution)/shard_map/dot_general | solution.py:28
  149.9 16.9 %all_to_all.26 = bf16[4,64,2048]{2,1,0:T(8,128)(2,1)S(1)} all-to-all(bf16[4,64,2048]{2,1,0:T(8,128)(2,1)S(1)} %bitcast.86), channel_id=1, replica_groups=mesh['dp'=8,'expert'=4] {'expert'}, dimensions={0} | all-to-all | bytes 2097152 | tf_op jit(solution)/shard_map/all_to_all | solution.py:120
  166.7 2.5 gather_fusion.3
  169.2 2.2 gather.29
  171.5 5.6 %convert_reduce_fusion = f32[128,2048]{1,0:T(8,128)S(1)} fusion(bf16[128,4,2048]{2,1,0:T(4,128)(2,1)} %gather.29, pred[128,4]{1,0:T(8,128)(4,1)S(1)} %copy-done.6), kind=kLoop, calls=%fused_computation.18 | loop fusion | flops 2883584 | bytes 3146240 | tf_op jit(solution)/shard_map/reduce_sum | solution.py:148
  177.1 1.1 fusion.21
  178.2 20.7 %all-reduce.5.cloned.1.call-done = f32[2048,128]{0,1:T(8,128)} async-done(((f32[2048,128]{0,1:T(8,128)}), f32[2048,128]{0,1:T(8,128)}) %all-reduce.5.cloned.1.call-update) | async-done | bytes 1048592 | tf_op jit(solution)/shard_map/psum | solution.py:156
  198.9 2.5 copy.55
  201.4 119.3 %reduce-scatter.5.cloned.1.call-done = bf16[1,192,2048]{2,1,0:T(8,128)(2,1)} async-done(((bf16[1,1536,2048]{2,1,0:T(8,128)(2,1)}), bf16[1,192,2048]{2,1,0:T(8,128)(2,1)}) %reduce-scatter.5.cloned.1.call-update) | async-done | bytes 786448 | tf_op jit(solution)/shard_map/reduce_scatter | solution.py:163
  320.7 210.8 %reduce-scatter.3.cloned.1.call-done = bf16[1,256,3072]{2,1,0:T(8,128)(2,1)} async-done(((bf16[1,2048,3072]{2,1,0:T(8,128)(2,1)}), bf16[1,256,3072]{2,1,0:T(8,128)(2,1)}) %reduce-scatter.3.cloned.1.call-update) | async-done | bytes 1572880 | tf_op jit(solution)/shard_map/reduce_scatter | solution.py:160
  (74 shorter events, 3.5 us)
Async XLA Ops:
  7.2 10.9 %copy-start = (bf16[128,2048]{1,0:T(8,128)(2,1)S(1)}, bf16[128,2048]{1,0:T(8,128)(2,1)}, u32[]{:S(2)}) copy-start(bf16[128,2048]{1,0:T(8,128)(2,1)} %param.7) | copy-start | bytes 1572868
  9.8 0.6 copy-start.5
  17.4 0.7 copy-start.10
  18.1 1.4 copy-start.2
  22.4 4.4 copy-start.3
  22.4 4.9 copy-start.7
  22.4 5.1 copy-start.12
  22.4 18.8 %all-to-all-start.2 = ((bf16[4,64,2048]{2,1,0:T(8,128)(2,1)}), bf16[4,64,2048]{2,1,0:T(8,128)(2,1)S(1)}, u32[]{:S(2)}, u32[]{:S(2)}) async-start(bf16[4,64,2048]{2,1,0:T(8,128)(2,1)} %get-tuple-element.38), calls=%async_computation.2 | async-start | bytes 2097152 | tf_op jit(solution)/shard_map/all_to_all | solution.py:79
  27.2 44.3 %copy-start.8 = (s32[1024]{0:T(1024)}, s32[1024]{0:T(1024)S(1)}, u32[]{:S(2)}) copy-start(s32[1024]{0:T(1024)S(1)} %pad_clamp_fusion) | copy-start | bytes 12292
  41.2 17.9 %all-to-all-start.1 = ((bf16[4,64,2048]{2,1,0:T(8,128)(2,1)}), bf16[4,64,2048]{2,1,0:T(8,128)(2,1)S(1)}, u32[]{:S(2)}, u32[]{:S(2)}) async-start(bf16[4,64,2048]{2,1,0:T(8,128)(2,1)} %get-tuple-element.39), calls=%async_computation.1 | async-start | bytes 2097152 | tf_op jit(solution)/shard_map/all_to_all | solution.py:86
  64.6 6.9 %all-to-all-start.4 = ((bf16[4,64,2]{1,2,0:T(2,128)(2,1)}), bf16[4,64,2]{1,2,0:T(2,128)(2,1)S(1)}, u32[]{:S(2)}, u32[]{:S(2)}) async-start(bf16[4,64,2]{1,2,0:T(2,128)(2,1)} %copy.51), calls=%async_computation.4 | async-start | bytes 4096 | tf_op jit(solution)/shard_map/all_to_all | solution.py:127
  67.8 48.7 %all-reduce.3.cloned.1.call-start = ((), (), s32[]{:S(2)}) async-start(), calls=%async_computation.7 | async-start | bytes 2097152 | tf_op jit(solution)/shard_map/psum | solution.py:156
  76.0 5.5 %copy-start.11 = (pred[256]{0:T(512)(128)(4,1)S(1)}, pred[256]{0:T(512)(128)(4,1)}, u32[]{:S(2)}) copy-start(pred[256]{0:T(512)(128)(4,1)} %copy-done.10) | copy-start | bytes 772
  79.1 119.8 %all-reduce.5.cloned.1.call-start = ((), (), s32[]{:S(2)}) async-start(), calls=%async_computation.8 | async-start | bytes 2097152 | tf_op jit(solution)/shard_map/psum | solution.py:156
  116.6 204.2 %reduce-scatter.5.cloned.1.call-start = ((), (), s32[]{:S(2)}) async-start(), calls=%async_computation.10 | async-start | bytes 7077888 | tf_op jit(solution)/shard_map/reduce_scatter | solution.py:163
  128.7 402.7 %reduce-scatter.3.cloned.1.call-start = ((), (), s32[]{:S(2)}) async-start(), calls=%async_computation.9 | async-start | bytes 14155776 | tf_op jit(solution)/shard_map/reduce_scatter | solution.py:160
  149.9 16.9 %copy-start.9 = (s32[1024]{0:T(1024)S(1)}, s32[1024]{0:T(1024)}, u32[]{:S(2)}) copy-start(s32[1024]{0:T(1024)} %copy-done.8) | copy-start | bytes 12292
  169.2 2.3 copy-start.6
  171.5 5.6 %copy-start.4 = (bf16[2048,128]{1,0:T(8,128)(2,1)S(1)}, bf16[2048,128]{1,0:T(8,128)(2,1)}, u32[]{:S(2)}) copy-start(bf16[2048,128]{1,0:T(8,128)(2,1)} %param.10) | copy-start | bytes 1572868
  171.5 360.0 %copy-start.1 = (bf16[128,2048]{1,0:T(8,128)(2,1)S(1)}, bf16[128,2048]{1,0:T(8,128)(2,1)}, u32[]{:S(2)}) copy-start(bf16[128,2048]{1,0:T(8,128)(2,1)} %param.7) | copy-start | bytes 1572868
Sparse Core Ops, SparseCore 0:
  79.2 37.2 all-reduce.2
  120.0 78.8 all-reduce.4
  203.1 117.6 reduce-scatter.4
  324.7 206.7 reduce-scatter.2
